TPU v7x, 32 devices: a whole 2x2x4 slice. The times are simulated.
32 devices in a mesh: groups: 2 (over y), seq: 4 (over z), batch: 2 (over x), head: 2 (over core).
Axes of the slice: x: 2, y: 2, z: 4, core: 2. Of those that a mesh axis runs over, the one named last changes fastest.
Arguments:
- hidden_in: bfloat16 [64, 4096], P(('groups', 'batch'), 'seq'), parts along dimension 0, may hold values from -400 to 400
- norm_gain_vector: bfloat16 [4096], P('seq'), may hold values from 0.099609375 to 1.8984375
- w_query: bfloat16 [4096, 4096], P('seq', 'head'), may hold values from -0.09375 to 0.09375
- key_cache_rows: bfloat16 [64, 4096, 128], P(('groups', 'batch'), 'seq'), parts along dimension 0, may hold values from -360 to 360
- value_cache_rows: bfloat16 [64, 4096, 128], P(('groups', 'batch'), 'seq'), parts along dimension 0, may hold values from -6 to 6
- k_new: bfloat16 [64, 128], P(('groups', 'batch')), parts along dimension 0, may hold values from -360 to 360
- v_new: bfloat16 [64, 128], P(('groups', 'batch')), parts along dimension 0, may hold values from -6 to 6
- lengths: int32 [64], P(('groups', 'batch')), parts along dimension 0, may hold values from 1 to 4096, as said below
- w_out: bfloat16 [4096, 4096], P('head', 'seq'), may hold values from -0.09375 to 0.09375
Outputs:
- layer_out: float32 [64, 4096], P(('groups', 'batch'), ('seq', 'head')), parts along dimension 0
There are 2 independent parts, one for each index of `groups`. A program takes and returns all parts, laid end to end along the dimension named above; an argument that names none is the same for every part. Nothing has to cross between parts.
Inputs may be any that keep to these rules, and one draw needn't show every extreme that they name: `lengths`: every sequence has at least one cached position; some sequence of each draw uses all 4096.
All inputs are finite; a program needn't handle non-finite values.
Results may differ from a plain program's by a relative error of at most 0.008.
Values sent between devices are 32-bit elements; how exact they have to be, the bound alone decides.
A program may use at most 64 MiB of HBM per device.

v0:
```python
import jax
import jax.numpy as jnp
from jax import lax
from jax.sharding import PartitionSpec as P

D = 4096
HD = 128


def combined_all(value, axis, join):
    pieces = jax.tree.map(lambda part: lax.all_gather(part, axis), value)
    head = jax.tree.map(lambda part: part[0], pieces)
    tail = jax.tree.map(lambda part: part[1:], pieces)
    total, _ = lax.scan(lambda total, share: (join(total, share), None), head, tail)
    return total


def combine(earlier, later):
    top_a, total_a, summed_a = earlier
    top_b, total_b, summed_b = later
    top = jnp.maximum(top_a, top_b)
    factor_a = jnp.exp(top_a - top)
    factor_b = jnp.exp(top_b - top)
    return (
        top,
        total_a * factor_a + total_b * factor_b,
        summed_a * factor_a[..., None] + summed_b * factor_b[..., None],
    )


def shards(
    hidden_in,
    norm_gain_vector,
    w_query,
    key_cache_rows,
    value_cache_rows,
    k_new,
    v_new,
    lengths,
    w_out,
):
    inputs = hidden_in.astype(jnp.float32)
    squares = lax.psum(jnp.sum(inputs * inputs, axis=-1), "seq")
    inv_rms = lax.rsqrt(squares / D + 1e-05)
    normed = (inputs * inv_rms[:, None] * norm_gain_vector.astype(jnp.float32)[None, :]).astype(
        jnp.bfloat16
    )
    partial_query = jnp.dot(normed, w_query, preferred_element_type=jnp.float32)
    inverse_root_norm = 1.0 / HD**0.5
    query_vectors = (lax.psum(partial_query, "seq") * inverse_root_norm).astype(jnp.bfloat16)
    seq_rows = query_vectors.shape[0]
    query_vectors = query_vectors.reshape(seq_rows, query_vectors.shape[1] // HD, HD)
    block_len = key_cache_rows.shape[1]
    scores = jnp.einsum(
        "irm,iam->ira", query_vectors, key_cache_rows, preferred_element_type=jnp.float32
    )
    own = jnp.einsum("bhd,bd->bh", query_vectors, k_new, preferred_element_type=jnp.float32)
    positions = lax.axis_index("seq") * block_len + lax.iota(jnp.int32, block_len)
    live_mask = (positions[None, :] < lengths[:, None])[:, None, :]
    local_top = jnp.maximum(jnp.max(jnp.where(live_mask, scores, -jnp.inf), axis=-1), own)
    softmax_weights = jnp.where(live_mask, jnp.exp(scores - local_top[..., None]), jnp.float32(0.0))
    local_total = jnp.sum(softmax_weights, axis=-1)
    local_partial_sum = jnp.einsum(
        "ajq,aqe->aje",
        softmax_weights.astype(jnp.bfloat16),
        value_cache_rows,
        preferred_element_type=jnp.float32,
    )
    top, totals, summed = combined_all((local_top, local_total, local_partial_sum), "seq", combine)
    fresh = jnp.exp(own - top)
    totals = totals + fresh
    result = (summed + fresh[..., None] * v_new.astype(jnp.float32)[:, None, :]) / totals[..., None]
    attended = result.astype(jnp.bfloat16).reshape(seq_rows, -1)
    partial_out = jnp.dot(attended, w_out, preferred_element_type=jnp.float32)
    return lax.psum_scatter(partial_out, "head", scatter_dimension=1, tiled=True)


def solution(mesh):
    placed = (
        P(("groups", "batch"), "seq"),
        P("seq"),
        P("seq", "head"),
        P(("groups", "batch"), "seq", None),
        P(("groups", "batch"), "seq", None),
        P(("groups", "batch"), None),
        P(("groups", "batch"), None),
        P(("groups", "batch")),
        P("head", "seq"),
    )
    return jax.shard_map(
        shards,
        mesh=mesh,
        in_specs=placed,
        out_specs=P(("groups", "batch"), ("seq", "head")),
        check_vma=False,
    )
```

profile of v0, /device:TPU:1, one launch (start us, length us, event | category | flops | bytes accessed | tf_op | source)
XLA Modules:
  0.0 123.6 jit_solution(10203687832632314913)
XLA Ops:
  6.5 0.9 fusion.10
  7.5 10.8 %psum.14 = f32[16]{0:T(128)S(1)} all-reduce(f32[16]{0:T(128)S(1)} %fusion.10), channel_id=1, replica_groups=mesh['groups'=2,'seq'=4,'batch'=2,'head'=2] {'seq'}, use_global_device_ids=true, to_apply=%region_1.0 | all-reduce | flops 16 | bytes 128 | tf_op jit(solution)/shard_map/psum | solution.py:43
  18.2 0.7 convert_element_type.22
  18.9 3.6 %fusion.17 = f32[16,2048]{1,0:T(8,128)} fusion(bf16[1024,2048]{1,0:T(8,128)(2,1)} %param.13, bf16[16,1024]{1,0:T(8,128)(2,1)} %param.11, f32[1024]{0:T(1024)S(1)} %convert_element_type.22, f32[16]{0:T(128)S(1)} %add_rsqrt_fusion), kind=kOutput, calls=%fused_computation.27 | convolution fusion | flops 67174400 | bytes 4362304 | tf_op jit(solution)/shard_map/dot_general | solution.py:48
  22.5 0.0 all-reduce.2.cloned.1.call-update
  22.5 0.0 reduce-scatter.2.cloned.1.call-start
  22.6 0.1 broadcast_compare_fusion
  22.7 32.8 %all-reduce.2.cloned.1.call-done = f32[16,2048]{1,0:T(8,128)} async-done(((f32[16,2048]{1,0:T(8,128)}), f32[16,2048]{1,0:T(8,128)}) %all-reduce.2.cloned.1.call-update) | async-done | bytes 131088 | tf_op jit(solution)/shard_map/psum | solution.py:50
  55.5 1.1 fusion.13
  56.6 0.1 fusion.21
  56.7 3.5 %select_reduce_fusion = (f32[16,16]{1,0:T(8,128)S(1)}, f32[16,16,1024]{2,1,0:T(8,128)S(1)}) fusion(pred[16,1024]{1,0:T(8,128)(4,1)S(1)} %broadcast_compare_fusion, bf16[16,16,128]{2,1,0:T(8,128)(2,1)S(1)} %bitcast.42, bf16[16,1024,128]{2,1,0:T(8,128)(2,1)} %param.14), kind=kOutput, calls=%fused_computation.9 | convolution fusion | flops 67632896 | bytes 5325824 | tf_op jit(solution)/shard_map/irm,iam->ira/dot_general | solution.py:54
  60.3 10.3 %all-gather = f32[64,16]{1,0:T(8,128)S(1)} all-gather(f32[16,16]{1,0:T(8,128)S(1)} %max.6), channel_id=2, replica_groups=mesh['groups'=2,'seq'=4,'batch'=2,'head'=2] {'seq'}, dimensions={0}, use_global_device_ids=true | all-gather | bytes 5120 | tf_op jit(solution)/shard_map/all_gather | solution.py:11
  70.5 0.3 fusion.4
  70.9 10.3 %all-gather.1 = f32[64,16]{1,0:T(8,128)S(1)} all-gather(f32[16,16]{1,0:T(8,128)S(1)} %fusion.4), channel_id=3, replica_groups=mesh['groups'=2,'seq'=4,'batch'=2,'head'=2] {'seq'}, dimensions={0}, use_global_device_ids=true | all-gather | bytes 5120 | tf_op jit(solution)/shard_map/all_gather | solution.py:11
  81.1 0.8 fusion.5
  81.9 11.8 %all-gather.2 = f32[64,16,128]{2,1,0:T(8,128)S(1)} all-gather(f32[16,16,128]{2,1,0:T(8,128)S(1)} %fusion.5), channel_id=4, replica_groups=mesh['groups'=2,'seq'=4,'batch'=2,'head'=2] {'seq'}, dimensions={0}, use_global_device_ids=true | all-gather | bytes 655360 | tf_op jit(solution)/shard_map/all_gather | solution.py:11
  93.8 0.6 while.14
  93.8 0.2 fusion.35
  94.0 0.2 fusion.35
  94.2 0.2 fusion.35
  94.4 0.1 divide_convert_fusion
  94.6 3.5 %fusion.14 = f32[16,1024]{1,0:T(8,128)} fusion(bf16[2048,1024]{1,0:T(8,128)(2,1)} %param.19, bf16[2,8,16,128]{3,2,1,0:T(8,128)(2,1)S(1)} %bitcast.40), kind=kOutput, calls=%fused_computation.24 | convolution fusion | flops 67108864 | bytes 4325376 | tf_op jit(solution)/shard_map/dot_general | solution.py:74
  98.0 0.0 reduce-scatter.2.cloned.1.call-update
  98.1 18.7 %reduce-scatter.2.cloned.1.call-done = f32[16,512]{1,0:T(8,128)} async-done(((f32[16,1024]{1,0:T(8,128)}), f32[16,512]{1,0:T(8,128)}) %reduce-scatter.2.cloned.1.call-update) | async-done | bytes 32784 | tf_op jit(solution)/shard_map/reduce_scatter | solution.py:75
  (24 shorter events, 0.2 us)
Async XLA Ops:
  6.5 50.0 %copy-start = (bf16[16,128]{1,0:T(8,128)(2,1)S(1)}, bf16[16,128]{1,0:T(8,128)(2,1)}, u32[]{:S(2)}) copy-start(bf16[16,128]{1,0:T(8,128)(2,1)} %param.16) | copy-start | bytes 12292
  6.5 16.0 %copy-start.2 = (bf16[16,128]{1,0:T(8,128)(2,1)S(1)}, bf16[16,128]{1,0:T(8,128)(2,1)}, u32[]{:S(2)}) copy-start(bf16[16,128]{1,0:T(8,128)(2,1)} %param.17) | copy-start | bytes 12292
  6.5 16.1 %copy-start.3 = (s32[16]{0:T(128)S(1)}, s32[16]{0:T(128)}, u32[]{:S(2)}) copy-start(s32[16]{0:T(128)} %param.18) | copy-start | bytes 196
  6.5 48.9 %all-reduce.2.cloned.1.call-start = ((), (), s32[]{:S(2)}) async-start(), calls=%async_computation.1 | async-start | bytes 262144 | tf_op jit(solution)/shard_map/psum | solution.py:50
  22.5 94.2 %reduce-scatter.2.cloned.1.call-start = ((), (), s32[]{:S(2)}) async-start(), calls=%async_computation.2 | async-start | bytes 98304 | tf_op jit(solution)/shard_map/reduce_scatter | solution.py:75
  55.5 25.7 %copy-start.1 = (bf16[16,1024,128]{2,1,0:T(8,128)(2,1)S(1)}, bf16[16,1024,128]{2,1,0:T(8,128)(2,1)}, u32[]{:S(2)}) copy-start(bf16[16,1024,128]{2,1,0:T(8,128)(2,1)} %param.15) | copy-start | bytes 12582916
Sparse Core Ops, SparseCore 0:
  22.6 32.7 all-reduce.1
  98.2 18.5 reduce-scatter.1
where the time goes:
time: 124 us
  waiting for transfers between devices  51.5 us (42%)
  blocking collectives  43.1 us (35%)
  between operations  13.5 us (11%)
  matrix products  11.5 us (9%)
  other arithmetic  3.82 us (3%)
    psum x1, waiting for transfers between devices, shards(): lax.psum(partial_query, 'seq') * inverse_root_norm  32.8 us
    all_gather x3, blocking collectives, combined_all(): pieces = jax.tree.map(lambda part: lax.all_gather(part, axis), value)  32.3 us
    reduce_scatter x1, waiting for transfers between devices, shards(): lax.psum_scatter(partial_out, 'head', scatter_dimension=1, tiled=True)  18.7 us
    psum x1, blocking collectives, shards(): squares = lax.psum(jnp.sum(inputs * inputs, axis=-1), 'seq')  10.8 us
    dot_general x1, matrix products, shards(): partial_query = jnp.dot(normed, w_query, preferred_element_type=jnp.float32)  3.56 us
    dot_general x1, matrix products, shards(): jnp.einsum('irm,iam->ira', query_vectors, key_cache_rows, preferred_eleme...  3.54 us
    dot_general x1, matrix products, shards(): partial_out = jnp.dot(attended, w_out, preferred_element_type=jnp.float32)  3.47 us
  transfers between devices with their start and end apart: 2, of which 2 were waited for; matrix products, arithmetic and copies ran while one was open for 0% of the time, Pallas kernels for 0%

commit v1 on v0

v1 whole, which is shorter than its diff:
```python
import functools

import jax
import jax.numpy as jnp
from jax import lax
from jax.experimental import pallas as pl
from jax.experimental.pallas import tpu as pltpu
from jax.sharding import PartitionSpec as P

HD = 128
EPS = 1e-05
MESH = pl.DeviceIdType.MESH
F32 = jnp.float32
BF16 = jnp.bfloat16


def chunk_edges(heads, cuts):
    step = heads // cuts
    return [(c * step, (c + 1) * step) for c in range(cuts)]


def kernel(
    n,
    heads,
    rows,
    cuts,
    lens_ref,
    hidden_hbm,
    gain_hbm,
    wq_hbm,
    keys_hbm,
    values_hbm,
    knew_hbm,
    vnew_hbm,
    wout_hbm,
    out_ref,
    hid,
    gain,
    wq,
    kbuf,
    vbuf,
    knew,
    vnew,
    wout,
    newf,
    qsend,
    qrecv,
    qall,
    asend,
    arecv,
    att,
    hsend,
    hrecv,
    small_sem,
    wq_sem,
    k_sem,
    v_sem,
    wo_sem,
    qs_send,
    qs_recv,
    qg_send,
    qg_recv,
    as_send,
    as_recv,
    ag_send,
    ag_recv,
    h_send,
    h_recv,
):
    me = lax.axis_index("seq")
    core = lax.axis_index("head")
    share = rows // n
    block = keys_hbm.shape[1]
    width = wq_hbm.shape[0] * n
    edges = chunk_edges(heads, cuts)

    small = [
        pltpu.make_async_copy(src, dst, small_sem.at[i])
        for i, (src, dst) in enumerate(
            ((hidden_hbm, hid), (gain_hbm, gain), (knew_hbm, knew), (vnew_hbm, vnew))
        )
    ]
    for copy in small:
        copy.start()
    wq_copies = []
    for c, (lo, hi) in enumerate(edges):
        cols = pl.ds(lo * HD, (hi - lo) * HD)
        wq_copies.append(pltpu.make_async_copy(wq_hbm.at[:, cols], wq.at[:, cols], wq_sem.at[c]))
        wq_copies[-1].start()
    owners = [lax.rem(me - k + n, n) for k in range(n)]
    k_copies, v_copies = [], []
    for k in range(n):
        group = pl.ds(owners[k] * share, share)
        k_copies.append(pltpu.make_async_copy(keys_hbm.at[group], kbuf.at[k], k_sem.at[k]))
        v_copies.append(pltpu.make_async_copy(values_hbm.at[group], vbuf.at[k], v_sem.at[k]))
        k_copies[-1].start()
        v_copies[-1].start()
    half = wout_hbm.shape[1] // 2
    wo_copies = []
    for i, side in enumerate((1 - core, core)):
        cols = pl.ds(pl.multiple_of(side * half, HD), half)
        wo_copies.append(pltpu.make_async_copy(wout_hbm.at[:, cols], wout.at[i], wo_sem.at[i]))
        wo_copies[-1].start()

    barrier = pltpu.get_barrier_semaphore()
    for k in range(1, n):
        pl.semaphore_signal(
            barrier, inc=1, device_id={"seq": lax.rem(me + k, n)}, device_id_type=MESH
        )
    pl.semaphore_signal(barrier, inc=1, device_id={"head": 1 - core}, device_id_type=MESH)

    small[0].wait()
    small[1].wait()
    x = hid[...].astype(F32)
    squares = jnp.sum(x * x, axis=-1, keepdims=True)
    scaled = x * gain[...].astype(F32)
    upper = scaled.astype(BF16)
    lower = (scaled - upper.astype(F32)).astype(BF16)
    both = jnp.concatenate([upper, lower], axis=0)
    for p in range(n):
        qsend[p, 0] = jnp.broadcast_to(squares[p * share : (p + 1) * share], (share, HD))
    qs = [[None] * n for _ in edges]
    for c, (lo, hi) in enumerate(edges):
        wq_copies[c].wait()
        product = jnp.dot(both, wq[:, lo * HD : hi * HD], preferred_element_type=F32)
        part = product[:rows] + product[rows:]
        for h in range(lo, hi):
            for p in range(n):
                qsend[p, h + 1] = part[
                    p * share : (p + 1) * share, (h - lo) * HD : (h - lo + 1) * HD
                ]
        if c == 0:
            pl.semaphore_wait(barrier, n)
        first = 0 if c == 0 else lo + 1
        span = pl.ds(first, hi + 1 - first)
        for k in range(1, n):
            peer = lax.rem(me + k, n)
            qs[c][k] = pltpu.make_async_remote_copy(
                src_ref=qsend.at[peer, span],
                dst_ref=qrecv.at[k - 1, span],
                send_sem=qs_send.at[c, k - 1],
                recv_sem=qs_recv.at[c, k - 1],
                device_id={"seq": peer},
                device_id_type=MESH,
            )
            qs[c][k].start()

    small[2].wait()
    small[3].wait()
    newf[0] = knew[...].astype(F32)
    newf[1] = vnew[...].astype(F32)

    for c in range(len(edges)):
        for k in range(1, n):
            qs[c][k].wait_recv()
    total = qsend[me]
    for k in range(1, n):
        total = total + qrecv[k - 1]
    inv = lax.rsqrt(total[0] / width + EPS) * (1.0 / HD**0.5)
    query = (total[1:] * inv[None]).astype(BF16).astype(F32)
    for r in range(share):
        qall[0, r] = jnp.concatenate([query[h, r : r + 1] for h in range(heads)], axis=0)
    qg = [None] * n
    for k in range(1, n):
        qg[k] = pltpu.make_async_remote_copy(
            src_ref=qall.at[0],
            dst_ref=qall.at[k],
            send_sem=qg_send.at[k - 1],
            recv_sem=qg_recv.at[k - 1],
            device_id={"seq": lax.rem(me + k, n)},
            device_id_type=MESH,
        )
        qg[k].start()

    lanes = lax.broadcasted_iota(jnp.int32, (heads, HD), 1)
    positions = me * block + lax.broadcasted_iota(jnp.int32, (heads, block), 1)
    sends = [None] * n
    for k in range(n):
        if k:
            qg[k].wait_recv()
        k_copies[k].wait()
        scores, own = [], []
        for r in range(share):
            q = qall[k, r]
            scores.append(
                lax.dot_general(
                    q.astype(BF16),
                    kbuf[k, r],
                    (((1,), (1,)), ((), ())),
                    preferred_element_type=F32,
                )
            )
            own.append(
                jnp.sum(q * newf[0, pl.ds(owners[k] * share + r, 1)], axis=-1, keepdims=True)
            )
        v_copies[k].wait()
        stats = jnp.zeros((heads, HD), F32)
        for r in range(share):
            live = positions < lens_ref[owners[k] * share + r]
            masked = jnp.where(live, scores[r], -jnp.inf)
            top = jnp.maximum(jnp.max(masked, axis=-1, keepdims=True), own[r])
            weights = jnp.exp(masked - top)
            stats = jnp.where(lanes == 2 * r, top, stats)
            stats = jnp.where(lanes == 2 * r + 1, jnp.sum(weights, axis=-1, keepdims=True), stats)
            asend[k, r] = jnp.dot(weights.astype(BF16), vbuf[k, r], preferred_element_type=F32)
        asend[k, share] = stats
        if k:
            sends[k] = pltpu.make_async_remote_copy(
                src_ref=asend.at[k],
                dst_ref=arecv.at[k - 1],
                send_sem=as_send.at[k - 1],
                recv_sem=as_recv.at[k - 1],
                device_id={"seq": owners[k]},
                device_id_type=MESH,
            )
            sends[k].start()

    for k in range(1, n):
        sends[k].wait_recv()
    stats = [asend[0, share]] + [arecv[k - 1, share] for k in range(1, n)]
    for r in range(share):
        tops = [s[:, 2 * r : 2 * r + 1] for s in stats]
        own = jnp.sum(qall[0, r] * newf[0, pl.ds(me * share + r, 1)], axis=-1, keepdims=True)
        top = functools.reduce(jnp.maximum, tops)
        fresh = jnp.exp(own - top)
        totals = fresh
        summed = fresh * newf[1, pl.ds(me * share + r, 1)]
        for k in range(n):
            factor = jnp.exp(tops[k] - top)
            totals = totals + stats[k][:, 2 * r + 1 : 2 * r + 2] * factor
            summed = summed + (asend[0, r] if k == 0 else arecv[k - 1, r]) * factor
        att[me * share + r] = (summed / totals).astype(BF16).astype(F32)
    ag = [None] * n
    mine = att.at[pl.ds(me * share, share)]
    for k in range(1, n):
        ag[k] = pltpu.make_async_remote_copy(
            src_ref=mine,
            dst_ref=mine,
            send_sem=ag_send.at[k - 1],
            recv_sem=ag_recv.at[k - 1],
            device_id={"seq": lax.rem(me + k, n)},
            device_id_type=MESH,
        )
        ag[k].start()
    for copy in wo_copies:
        copy.wait()
    for k in range(1, n):
        ag[k].wait_recv()

    attended = jnp.concatenate([att[:, h, :] for h in range(heads)], axis=1).astype(BF16)
    hsend[...] = jnp.dot(attended, wout[0], preferred_element_type=F32)
    swap = pltpu.make_async_remote_copy(
        src_ref=hsend,
        dst_ref=hrecv,
        send_sem=h_send,
        recv_sem=h_recv,
        device_id={"head": 1 - core},
        device_id_type=MESH,
    )
    swap.start()
    kept = jnp.dot(attended, wout[1], preferred_element_type=F32)
    swap.wait_recv()
    out_ref[...] = kept + hrecv[...]

    for k in range(1, n):
        for c in range(len(edges)):
            qs[c][k].wait_send()
        qg[k].wait_send()
        sends[k].wait_send()
        ag[k].wait_send()
    swap.wait_send()


def solution(mesh):
    n = mesh.shape["seq"]
    cuts = 2

    def shards(hidden, gain, wq, keys, values, knew, vnew, lengths, wout):
        rows, depth = hidden.shape
        heads = wq.shape[1] // HD
        share = rows // n
        block = keys.shape[1]
        half = wout.shape[1] // 2
        anywhere = pl.BlockSpec(memory_space=pl.ANY)
        dma = pltpu.SemaphoreType.DMA
        return pl.pallas_call(
            functools.partial(kernel, n, heads, rows, cuts),
            out_shape=jax.ShapeDtypeStruct((rows, half), F32),
            in_specs=[pl.BlockSpec(memory_space=pltpu.SMEM)] + [anywhere] * 8,
            out_specs=pl.BlockSpec(memory_space=pltpu.VMEM),
            scratch_shapes=[
                pltpu.VMEM((rows, depth), BF16),
                pltpu.VMEM((1, depth), BF16),
                pltpu.VMEM(wq.shape, BF16),
                pltpu.VMEM((n, share, block, HD), BF16),
                pltpu.VMEM((n, share, block, HD), BF16),
                pltpu.VMEM((rows, HD), BF16),
                pltpu.VMEM((rows, HD), BF16),
                pltpu.VMEM((2, wout.shape[0], half), BF16),
                pltpu.VMEM((2, rows, HD), F32),
                pltpu.VMEM((n, heads + 1, share, HD), F32),
                pltpu.VMEM((n - 1, heads + 1, share, HD), F32),
                pltpu.VMEM((n, share, heads, HD), F32),
                pltpu.VMEM((n, share + 1, heads, HD), F32),
                pltpu.VMEM((n - 1, share + 1, heads, HD), F32),
                pltpu.VMEM((rows, heads, HD), F32),
                pltpu.VMEM((rows, half), F32),
                pltpu.VMEM((rows, half), F32),
                dma((4,)),
                dma((cuts,)),
                dma((n,)),
                dma((n,)),
                dma((2,)),
                dma((cuts, n - 1)),
                dma((cuts, n - 1)),
                dma((n - 1,)),
                dma((n - 1,)),
                dma((n - 1,)),
                dma((n - 1,)),
                dma((n - 1,)),
                dma((n - 1,)),
                dma(()),
                dma(()),
            ],
            compiler_params=pltpu.CompilerParams(collective_id=0, has_side_effects=True),
            name="decode_step",
        )(lengths, hidden, gain.reshape(1, -1), wq, keys, values, knew, vnew, wout)

    placed = (
        P(("groups", "batch"), "seq"),
        P("seq"),
        P("seq", "head"),
        P(("groups", "batch"), "seq", None),
        P(("groups", "batch"), "seq", None),
        P(("groups", "batch"), None),
        P(("groups", "batch"), None),
        P(("groups", "batch")),
        P("head", "seq"),
    )
    return jax.shard_map(
        shards,
        mesh=mesh,
        in_specs=placed,
        out_specs=P(("groups", "batch"), ("seq", "head")),
        check_vma=False,
    )
```

time: 124 us -> 31 us (0.25)
  waiting for transfers between devices: 51.5 us -> 0 us
  blocking collectives: 43.1 us -> 0 us
  Pallas kernels: 0 us -> 28.2 us
  between operations: 13.5 us -> 0.01 us
  matrix products: 11.5 us -> 0 us
  other arithmetic: 3.82 us -> 0 us
  local copies, waits for them, and re-layouts: 0.07 us -> 2.65 us
    psum x1 -> x0, waiting for transfers between devices: 32.8 us -> none  [shards(): lax.psum(partial_query, 'seq') * inverse_root_norm]
    all_gather x3 -> x0, blocking collectives: 32.3 us -> none  [combined_all(): pieces = jax.tree.map(lambda part: lax.all_gather(part, axis), value)]
    pallas_call x0 -> x1, Pallas kernels: none -> 28.2 us  [shards(): pl.pallas_call(functools.partial(kernel, n, heads, rows, cuts), out_shape...]
    reduce_scatter x1 -> x0, waiting for transfers between devices: 18.7 us -> none  [shards(): lax.psum_scatter(partial_out, 'head', scatter_dimension=1, tiled=True)]
    dot_general x5 -> x0, matrix products: 11.5 us -> none  [the longest x1 3.56 us: shards(): partial_query = jnp.dot(normed, w_query, preferred_element_type=jnp.float32)]
    psum x1 -> x0, blocking collectives: 10.8 us -> none  [shards(): squares = lax.psum(jnp.sum(inputs * inputs, axis=-1), 'seq')]
    unnamed x9 -> x1, local copies, waits for them, and re-layouts: 0.03 us -> 1.38 us
    reshape x0 -> x1, local copies, waits for them, and re-layouts: none -> 1.28 us  [shards(): gain.reshape(1, -1)]
  transfers between devices with their start and end apart: 2 -> 0, of which waited for: 2 -> 0; matrix products, arithmetic and copies ran while one was open for 0% -> 0% of each run, Pallas kernels for 0% -> 0%
where the time goes in v1:
time: 31 us; the launch traced here: 30.8 us
  Pallas kernels  28.2 us (91%)
  local copies, waits for them, and re-layouts  2.65 us (9%)
    pallas_call x1, Pallas kernels, shards(): pl.pallas_call(functools.partial(kernel, n, heads, rows, cuts), out_shape...  28.2 us
    unnamed x1, local copies, waits for them, and re-layouts  1.38 us
    reshape x1, local copies, waits for them, and re-layouts, shards(): gain.reshape(1, -1)  1.28 us

profile of v1, /device:TPU:1, one launch (start us, length us, event | category | flops | bytes accessed | tf_op | source)
XLA Modules:
  0.0 30.8 jit_solution(17264070108627142182)
XLA Ops:
  0.0 1.3 %reshape.3.gain_hbm = bf16[1,1024]{1,0:T(2,128)(2,1)} reshape(bf16[1024]{0:T(1024)(128)(2,1)} %param.10) | data formatting | bytes 4096 | tf_op jit(solution)/shard_map/reshape | solution.py:327
  1.3 28.2 %decode_step.1 = f32[16,512]{1,0:T(8,128)} custom-call(s32[16]{0:T(128)} %lens_ref.1, bf16[16,1024]{1,0:T(8,128)(2,1)} %hidden_hbm.1, bf16[1,1024]{1,0:T(2,128)(2,1)} %reshape.3.gain_hbm, bf16[1024,2048]{1,0:T(8,128)(2,1)} %wq_hbm.1, bf16[16,1024,128]{2,1,0:T(8,128)(2,1)} %keys_hbm.1, bf16[16,1024,128]{2,1,0:T(8,128)(2,1)} %values_hbm.1, ...), custom_call_target="tpu_custom_call" | custom-call | tf_op jit(solution)/shard_map/decode_step/pallas_call | solution.py:286
  29.5 1.4 %copy.11 = f32[16,512]{1,0:T(8,128)} copy(f32[16,512]{1,0:T(8,128)} %decode_step.1) | data formatting | bytes 65536

commit v2 on v1

v2 whole, which is shorter than its diff:
```python
import functools

import jax
import jax.numpy as jnp
from jax import lax
from jax.experimental import pallas as pl
from jax.experimental.pallas import tpu as pltpu
from jax.sharding import PartitionSpec as P

HD = 128
EPS = 1e-05
MESH = pl.DeviceIdType.MESH
F32 = jnp.float32
BF16 = jnp.bfloat16


def chunk_edges(heads, cuts):
    step = heads // cuts
    return [(c * step, (c + 1) * step) for c in range(cuts)]


def kernel(
    n,
    heads,
    rows,
    cuts,
    m,
    subs,
    lens_ref,
    hidden_hbm,
    gain_hbm,
    wq_hbm,
    keys_hbm,
    values_hbm,
    knew_hbm,
    vnew_hbm,
    wout_hbm,
    out_ref,
    hid,
    gain,
    wq,
    kbuf,
    vbuf,
    knew,
    vnew,
    wout,
    newf,
    qsend,
    qrecv,
    qturn,
    qall,
    asend,
    arecv,
    att,
    hsend,
    hrecv,
    small_sem,
    wq_sem,
    k_sem,
    v_sem,
    wo_sem,
    qs_send,
    qs_recv,
    qg_send,
    qg_recv,
    as_send,
    as_recv,
    ag_send,
    ag_recv,
    h_send,
    h_recv,
):
    me = lax.axis_index("seq")
    core = lax.axis_index("head")
    other = 1 - core
    first = (n - m) // 2
    share = rows // m
    piece = share // subs
    block = keys_hbm.shape[1]
    width = wq_hbm.shape[0] * n
    edges = chunk_edges(heads, cuts)
    owning = jnp.logical_and(me >= first, me < first + m)
    my_slot = jnp.clip(me - first, 0, m - 1)
    slots = [lax.rem(my_slot + k, m) for k in range(m)]
    away = [(n // 2 + k) % n for k in range(n)]
    away = [k for k in away if k]

    barrier = pltpu.get_barrier_semaphore()

    def greet(s):
        pl.semaphore_signal(
            barrier, inc=1, device_id={"seq": s, "head": core}, device_id_type=MESH
        )

    for s in range(n):
        meet = me != s
        if not first <= s < first + m:
            meet = jnp.logical_and(meet, owning)
        pl.when(meet)(functools.partial(greet, s))
    pl.semaphore_signal(barrier, inc=1, device_id={"head": other}, device_id_type=MESH)

    small = [
        pltpu.make_async_copy(src, dst, small_sem.at[i])
        for i, (src, dst) in enumerate(
            ((hidden_hbm, hid), (gain_hbm, gain), (knew_hbm, knew), (vnew_hbm, vnew))
        )
    ]
    for copy in small:
        copy.start()
    wq_copies = []
    for c, (lo, hi) in enumerate(edges):
        cols = pl.ds(lo * HD, (hi - lo) * HD)
        wq_copies.append(pltpu.make_async_copy(wq_hbm.at[:, cols], wq.at[:, cols], wq_sem.at[c]))
        wq_copies[-1].start()
    k_copies, v_copies = [], []
    for k in range(m):
        group = pl.ds(slots[k] * share, share)
        k_copies.append(pltpu.make_async_copy(keys_hbm.at[group], kbuf.at[k], k_sem.at[k]))
        v_copies.append(pltpu.make_async_copy(values_hbm.at[group], vbuf.at[k], v_sem.at[k]))
        k_copies[-1].start()
        v_copies[-1].start()
    half = wout_hbm.shape[1] // 2
    wo_copies = []
    for i, side in enumerate((other, core)):
        cols = pl.ds(pl.multiple_of(side * half, HD), half)
        wo_copies.append(pltpu.make_async_copy(wout_hbm.at[:, cols], wout.at[i], wo_sem.at[i]))
        wo_copies[-1].start()

    small[0].wait()
    small[1].wait()
    x = hid[...].astype(F32)
    squares = jnp.sum(x * x, axis=-1, keepdims=True)
    scaled = x * gain[...].astype(F32)
    upper = scaled.astype(BF16)
    lower = (scaled - upper.astype(F32)).astype(BF16)
    both = jnp.concatenate([upper, lower], axis=0)
    for p in range(m):
        qsend[p, 0] = jnp.broadcast_to(squares[p * share : (p + 1) * share], (share, HD))
    qs = [[None] * m for _ in edges]

    def arrivals(c, s):
        lo, hi = edges[c]
        span = pl.ds(0 if c == 0 else lo + 1, hi + 1 - (0 if c == 0 else lo + 1))
        return pltpu.make_async_remote_copy(
            src_ref=qsend.at[0, span],
            dst_ref=qrecv.at[s, span],
            send_sem=qs_send.at[c, 0],
            recv_sem=qs_recv.at[c, s],
            device_id={"seq": me, "head": core},
            device_id_type=MESH,
        )

    for c, (lo, hi) in enumerate(edges):
        wq_copies[c].wait()
        product = jnp.dot(both, wq[:, lo * HD : hi * HD], preferred_element_type=F32)
        part = product[:rows] + product[rows:]
        for h in range(lo, hi):
            for p in range(m):
                qsend[p, h + 1] = part[
                    p * share : (p + 1) * share, (h - lo) * HD : (h - lo + 1) * HD
                ]
        if c == 0:
            pl.semaphore_wait(barrier, jnp.where(owning, n, m + 1))
        start = 0 if c == 0 else lo + 1
        span = pl.ds(start, hi + 1 - start)
        for k in reversed(range(m)):
            qs[c][k] = pltpu.make_async_remote_copy(
                src_ref=qsend.at[slots[k], span],
                dst_ref=qrecv.at[me, span],
                send_sem=qs_send.at[c, k],
                recv_sem=qs_recv.at[c, me],
                device_id={"seq": slots[k] + first, "head": core},
                device_id_type=MESH,
            )
            if k:
                qs[c][k].start()
            else:
                pl.when(jnp.logical_not(owning))(qs[c][k].start)

    small[2].wait()
    small[3].wait()
    newf[0] = knew[...].astype(F32)
    newf[1] = vnew[...].astype(F32)

    def gathers(u):
        return [
            pltpu.make_async_remote_copy(
                src_ref=qall.at[my_slot, pl.ds(u * piece, piece)],
                dst_ref=qall.at[my_slot, pl.ds(u * piece, piece)],
                send_sem=qg_send.at[u, i],
                recv_sem=qg_recv.at[u, my_slot],
                device_id={"seq": lax.rem(me + k, n), "head": core},
                device_id_type=MESH,
            )
            for i, k in enumerate(away)
        ]

    @pl.when(owning)
    def _():
        for c in range(len(edges)):
            for s in range(1, n):
                arrivals(c, lax.rem(me + s, n)).wait_recv()
        total = qsend[my_slot]
        for s in range(1, n):
            total = total + qrecv[lax.rem(me + s, n)]
        inv = lax.rsqrt(total[0] / width + EPS) * (1.0 / HD**0.5)
        qturn[...] = (total[1:] * inv[None]).astype(BF16).astype(F32)
        for u in range(subs):
            for r in range(u * piece, (u + 1) * piece):
                qall[my_slot, r] = qturn[:, r, :]
            for copy in gathers(u):
                copy.start()

    lanes = lax.broadcasted_iota(jnp.int32, (heads, HD), 1)
    positions = me * block + lax.broadcasted_iota(jnp.int32, (heads, block), 1)
    sends = []
    for k in range(m):
        for u in range(subs):
            i = k * subs + u
            arrival = pltpu.make_async_remote_copy(
                src_ref=qall.at[my_slot, pl.ds(u * piece, piece)],
                dst_ref=qall.at[slots[k], pl.ds(u * piece, piece)],
                send_sem=qg_send.at[u, 0],
                recv_sem=qg_recv.at[u, slots[k]],
                device_id={"seq": me, "head": core},
                device_id_type=MESH,
            )
            if k:
                arrival.wait_recv()
            else:
                pl.when(jnp.logical_not(owning))(arrival.wait_recv)
            if u == 0:
                k_copies[k].wait()
            scores, own = [], []
            for r in range(piece):
                q = qall[slots[k], u * piece + r]
                scores.append(
                    lax.dot_general(
                        q.astype(BF16),
                        kbuf[k, u * piece + r],
                        (((1,), (1,)), ((), ())),
                        preferred_element_type=F32,
                    )
                )
                row = slots[k] * share + u * piece + r
                own.append(jnp.sum(q * newf[0, pl.ds(row, 1)], axis=-1, keepdims=True))
            if u == 0:
                v_copies[k].wait()
            stats = jnp.zeros((heads, HD), F32)
            for r in range(piece):
                live = positions < lens_ref[slots[k] * share + u * piece + r]
                masked = jnp.where(live, scores[r], -jnp.inf)
                top = jnp.maximum(jnp.max(masked, axis=-1, keepdims=True), own[r])
                weights = jnp.exp(masked - top)
                weight = jnp.sum(weights, axis=-1, keepdims=True)
                stats = jnp.where(lanes == 2 * r, top, stats)
                stats = jnp.where(lanes == 2 * r + 1, weight, stats)
                asend[i, r] = jnp.dot(
                    weights.astype(BF16), vbuf[k, u * piece + r], preferred_element_type=F32
                )
            asend[i, piece] = stats
            sends.append(
                pltpu.make_async_remote_copy(
                    src_ref=asend.at[i],
                    dst_ref=arecv.at[me, u],
                    send_sem=as_send.at[i],
                    recv_sem=as_recv.at[u, me],
                    device_id={"seq": slots[k] + first, "head": core},
                    device_id_type=MESH,
                )
            )
            if k:
                sends[-1].start()
            else:
                pl.when(jnp.logical_not(owning))(sends[-1].start)

    def returns(u):
        return [
            pltpu.make_async_remote_copy(
                src_ref=att.at[pl.ds(my_slot * share + u * piece, piece)],
                dst_ref=att.at[pl.ds(my_slot * share + u * piece, piece)],
                send_sem=ag_send.at[u, i],
                recv_sem=ag_recv.at[u, my_slot],
                device_id={"seq": lax.rem(me + k, n), "head": core},
                device_id_type=MESH,
            )
            for i, k in enumerate(away)
        ]

    @pl.when(owning)
    def _():
        for u in range(subs):
            others = [lax.rem(me + s, n) for s in range(1, n)]
            for s in others:
                pltpu.make_async_remote_copy(
                    src_ref=asend.at[0],
                    dst_ref=arecv.at[s, u],
                    send_sem=as_send.at[0],
                    recv_sem=as_recv.at[u, s],
                    device_id={"seq": me, "head": core},
                    device_id_type=MESH,
                ).wait_recv()
            stats = [asend[u, piece]] + [arecv[s, u, piece] for s in others]
            for r in range(piece):
                row = my_slot * share + u * piece + r
                tops = [s[:, 2 * r : 2 * r + 1] for s in stats]
                own = jnp.sum(
                    qall[my_slot, u * piece + r] * newf[0, pl.ds(row, 1)], axis=-1, keepdims=True
                )
                top = functools.reduce(jnp.maximum, tops)
                fresh = jnp.exp(own - top)
                totals = fresh
                summed = fresh * newf[1, pl.ds(row, 1)]
                for s in range(n):
                    factor = jnp.exp(tops[s] - top)
                    totals = totals + stats[s][:, 2 * r + 1 : 2 * r + 2] * factor
                    summed = summed + (arecv[others[s - 1], u, r] if s else asend[u, r]) * factor
                att[row] = (summed / totals).astype(BF16).astype(F32)
            for copy in returns(u):
                copy.start()

    for copy in wo_copies:
        copy.wait()
    for j in range(m):
        for u in range(subs):
            group = pl.ds(j * share + u * piece, piece)
            arrival = pltpu.make_async_remote_copy(
                src_ref=att.at[group],
                dst_ref=att.at[group],
                send_sem=ag_send.at[u, 0],
                recv_sem=ag_recv.at[u, j],
                device_id={"seq": me, "head": core},
                device_id_type=MESH,
            )
            pl.when(me != first + j)(arrival.wait_recv)

    attended = jnp.concatenate([att[:, h, :] for h in range(heads)], axis=1).astype(BF16)
    hsend[...] = jnp.dot(attended, wout[0], preferred_element_type=F32)
    swap = pltpu.make_async_remote_copy(
        src_ref=hsend,
        dst_ref=hrecv,
        send_sem=h_send,
        recv_sem=h_recv,
        device_id={"head": other},
        device_id_type=MESH,
    )
    swap.start()
    kept = jnp.dot(attended, wout[1], preferred_element_type=F32)
    swap.wait_recv()
    out_ref[...] = kept + hrecv[...]

    for c in range(len(edges)):
        for k in range(1, m):
            qs[c][k].wait_send()
    for copy in sends[subs:]:
        copy.wait_send()
    swap.wait_send()

    @pl.when(owning)
    def _():
        for u in range(subs):
            for copy in gathers(u) + returns(u):
                copy.wait_send()

    @pl.when(jnp.logical_not(owning))
    def _():
        for c in range(len(edges)):
            qs[c][0].wait_send()
        for copy in sends[:subs]:
            copy.wait_send()


def solution(mesh):
    n = mesh.shape["seq"]
    cuts = 2
    m = max(n // 2, 1)
    subs = 2

    def shards(hidden, gain, wq, keys, values, knew, vnew, lengths, wout):
        rows, depth = hidden.shape
        heads = wq.shape[1] // HD
        share = rows // m
        piece = share // subs
        block = keys.shape[1]
        half = wout.shape[1] // 2
        anywhere = pl.BlockSpec(memory_space=pl.ANY)
        dma = pltpu.SemaphoreType.DMA
        return pl.pallas_call(
            functools.partial(kernel, n, heads, rows, cuts, m, subs),
            out_shape=jax.ShapeDtypeStruct((rows, half), F32),
            in_specs=[pl.BlockSpec(memory_space=pltpu.SMEM)] + [anywhere] * 8,
            out_specs=pl.BlockSpec(memory_space=pltpu.VMEM),
            scratch_shapes=[
                pltpu.VMEM((rows, depth), BF16),
                pltpu.VMEM((1, depth), BF16),
                pltpu.VMEM(wq.shape, BF16),
                pltpu.VMEM((m, share, block, HD), BF16),
                pltpu.VMEM((m, share, block, HD), BF16),
                pltpu.VMEM((rows, HD), BF16),
                pltpu.VMEM((rows, HD), BF16),
                pltpu.VMEM((2, wout.shape[0], half), BF16),
                pltpu.VMEM((2, rows, HD), F32),
                pltpu.VMEM((m, heads + 1, share, HD), F32),
                pltpu.VMEM((n, heads + 1, share, HD), F32),
                pltpu.VMEM((heads, share, HD), F32),
                pltpu.VMEM((m, share, heads, HD), F32),
                pltpu.VMEM((m * subs, piece + 1, heads, HD), F32),
                pltpu.VMEM((n, subs, piece + 1, heads, HD), F32),
                pltpu.VMEM((rows, heads, HD), F32),
                pltpu.VMEM((rows, half), F32),
                pltpu.VMEM((rows, half), F32),
                dma((4,)),
                dma((cuts,)),
                dma((m,)),
                dma((m,)),
                dma((2,)),
                dma((cuts, m)),
                dma((cuts, n)),
                dma((subs, n)),
                dma((subs, m)),
                dma((m * subs,)),
                dma((subs, n)),
                dma((subs, n)),
                dma((subs, m)),
                dma(()),
                dma(()),
            ],
            compiler_params=pltpu.CompilerParams(collective_id=0, has_side_effects=True),
            name="decode_step",
        )(lengths, hidden, gain.reshape(1, -1), wq, keys, values, knew, vnew, wout)

    placed = (
        P(("groups", "batch"), "seq"),
        P("seq"),
        P("seq", "head"),
        P(("groups", "batch"), "seq", None),
        P(("groups", "batch"), "seq", None),
        P(("groups", "batch"), None),
        P(("groups", "batch"), None),
        P(("groups", "batch")),
        P("head", "seq"),
    )
    return jax.shard_map(
        shards,
        mesh=mesh,
        in_specs=placed,
        out_specs=P(("groups", "batch"), ("seq", "head")),
        check_vma=False,
    )
```

time: 31 us -> 30.2 us (0.974)
  Pallas kernels: 28.2 us -> 27.3 us
    pallas_call x1, Pallas kernels: 28.2 us -> 27.3 us  [shards(): pl.pallas_call(functools.partial(kernel, n, heads, rows, cuts, m, subs),...]
where the time goes in v2:
time: 30.2 us; the launch traced here: 30 us
  Pallas kernels  27.3 us (90%)
  local copies, waits for them, and re-layouts  2.65 us (9%)
    pallas_call x1, Pallas kernels, shards(): pl.pallas_call(functools.partial(kernel, n, heads, rows, cuts, m, subs),...  27.3 us
    unnamed x1, local copies, waits for them, and re-layouts  1.38 us
    reshape x1, local copies, waits for them, and re-layouts, shards(): gain.reshape(1, -1)  1.28 us

profile of v2, /device:TPU:1, one launch (start us, length us, event | category | flops | bytes accessed | tf_op | source)
XLA Modules:
  0.0 30.0 jit_solution(8356044066967496546)
XLA Ops:
  0.0 1.3 %reshape.3.gain_hbm = bf16[1,1024]{1,0:T(2,128)(2,1)} reshape(bf16[1024]{0:T(1024)(128)(2,1)} %param.10) | data formatting | bytes 4096 | tf_op jit(solution)/shard_map/reshape | solution.py:430
  1.3 27.3 %decode_step.1 = f32[16,512]{1,0:T(8,128)} custom-call(s32[16]{0:T(128)} %lens_ref.1, bf16[16,1024]{1,0:T(8,128)(2,1)} %hidden_hbm.1, bf16[1,1024]{1,0:T(2,128)(2,1)} %reshape.3.gain_hbm, bf16[1024,2048]{1,0:T(8,128)(2,1)} %wq_hbm.1, bf16[16,1024,128]{2,1,0:T(8,128)(2,1)} %keys_hbm.1, bf16[16,1024,128]{2,1,0:T(8,128)(2,1)} %values_hbm.1, ...), custom_call_target="tpu_custom_call" | custom-call | tf_op jit(solution)/shard_map/decode_step/pallas_call | solution.py:388
  28.6 1.4 %copy.11 = f32[16,512]{1,0:T(8,128)} copy(f32[16,512]{1,0:T(8,128)} %decode_step.1) | data formatting | bytes 65536
